TPU v7x, 32 devices: a whole 2x2x4 slice. The times are simulated.
32 devices in a mesh: dp: 4 (over z), row: 2 (over y), col: 4 (over x, core).
Axes of the slice: x: 2, y: 2, z: 4, core: 2. Of those that a mesh axis runs over, the one named last changes fastest.
Arguments:
- x_seq: bfloat16 [1024, 64, 576], P(('dp', 'row', 'col'))
- dy_seq: bfloat16 [1024, 64, 576], P(('dp', 'row', 'col'))
- w_query: bfloat16 [576, 9, 64], P(('row', 'col'))
- w_key: bfloat16 [576, 3, 64], P(('row', 'col'))
- w_value: bfloat16 [576, 3, 64], P(('row', 'col'))
- w_out: bfloat16 [9, 64, 576], P(None, None, ('row', 'col'))
- grad_next: float32 [32, 3, 576, 1536], P(('dp', 'row', 'col'))
Outputs:
- output 1: bfloat16 [1024, 64, 576], P(('dp', 'row', 'col'))
- output 2: float32 [3, 576, 1536], P(None, None, ('row', 'col'))
- output 3: float32 [32, 576, 9, 64], P(('dp', 'row', 'col'))
- output 4: float32 [32, 576, 3, 64], P(('dp', 'row', 'col'))
- output 5: float32 [32, 576, 3, 64], P(('dp', 'row', 'col'))
- output 6: float32 [32, 9, 64, 576], P(('dp', 'row', 'col'))
All inputs are finite; a program needn't handle non-finite values.
Results may differ from a plain program's by a relative error of at most 0.0105782.
Values are sent between devices in bfloat16 or wider.
A program may use at most 1 GiB of HBM per device.

v0:
```python
import functools
import jax, jax.numpy as jnp, numpy as np
from jax import lax
from jax.experimental import pallas as pl
from jax.experimental.pallas import tpu as pltpu
from jax.sharding import PartitionSpec as P

T = 2048
D = 576
HD = 64
F32 = jnp.float32
BF = jnp.bfloat16
LOG2E = 1.4426950408889634


def rope_tables():
    pos = np.arange(64, dtype=np.float32)
    inv = np.float32(10000.0) ** (-np.arange(32, dtype=np.float32) * np.float32(2.0 / 64))
    ang = inv[:, None] * pos[None, :]
    cos, sin = np.cos(ang).astype(np.float32), np.sin(ang).astype(np.float32)
    return np.stack([np.tile(cos, (1, 4)), np.tile(sin, (1, 4))])


def nt(a, b):
    return lax.dot_general(a, b, (((1,), (1,)), ((), ())), preferred_element_type=F32)


def nn(a, b):
    return lax.dot_general(a, b, (((1,), (0,)), ((), ())), preferred_element_type=F32)


def tn(a, b):
    return lax.dot_general(a, b, (((0,), (0,)), ((), ())), preferred_element_type=F32)


def project(i, w, x, dy, tab, qkvT, doT, kl, vl):
    rows = pl.ds(pl.multiple_of(i * 256, 256), 256)
    cos, sin = tab[0], tab[1]
    raw = nt(w[0:960, :], x[rows, :])
    for h in range(12):
        a, b = raw[64 * h:64 * h + 32], raw[64 * h + 32:64 * h + 64]
        qkvT[64 * h:64 * h + 32, rows] = (a * cos - b * sin).astype(BF)
        qkvT[64 * h + 32:64 * h + 64, rows] = (b * cos + a * sin).astype(BF)
    qkvT[768:960, rows] = raw[768:960].astype(BF)
    doT[:, rows] = nt(w[960:1536, :], dy[rows, :]).astype(BF)
    for g in range(3):
        for src, dst in ((576, kl), (768, vl)):
            tr = qkvT[src + 64 * g:src + 64 * g + 64, rows].T
            for s in range(2):
                keys = pl.ds(pl.multiple_of(i * 128 + 64 * s, 64), 64)
                dst[g, keys, :] = jnp.concatenate([tr[128 * s:128 * s + 64], tr[128 * s + 64:128 * s + 128]], axis=1)


def attend(j, tab, qkvT, doT, kl, vl, oT, dqkvT):
    cols = pl.ds(pl.multiple_of(j * 128, 128), 128)
    keys = pl.ds(pl.multiple_of(j * 64, 64), 64)
    cos, sin = tab[0, :, 0:128], tab[1, :, 0:128]
    key_i = lax.broadcasted_iota(jnp.int32, (64, 384), 0)
    lane = lax.broadcasted_iota(jnp.int32, (64, 384), 1)
    causal = key_i <= lane % 64
    first = lane % 128 < 64
    zero = jnp.zeros((64, 384), BF)

    def blocks(v):
        return jnp.concatenate([jnp.where(first, v, zero), jnp.where(first, zero, v)], axis=0)

    for g in range(3):
        heads = [64 * (3 * g + r) for r in range(3)]
        q3 = jnp.concatenate([qkvT[h:h + 64, cols] for h in heads], axis=1)
        do3 = jnp.concatenate([doT[h:h + 64, cols] for h in heads], axis=1)
        kT = qkvT[576 + 64 * g:640 + 64 * g, cols]
        vT = qkvT[768 + 64 * g:832 + 64 * g, cols]
        s = nn(kl[g, keys, :], blocks(q3)) * (0.125 * LOG2E)
        dp = nn(vl[g, keys, :], blocks(do3))
        s = jnp.where(causal, s, -1e30)
        e = jnp.exp2(s - jnp.max(s, axis=0, keepdims=True))
        p = e * (1.0 / jnp.sum(e, axis=0, keepdims=True))
        delta = jnp.sum(p * dp, axis=0, keepdims=True)
        ds = (p * (dp - delta) * 0.125).astype(BF)
        pbd, dsbd = blocks(p.astype(BF)), blocks(ds)
        o = nn(vT, pbd).astype(BF)
        dq = nn(kT, dsbd)
        for r in range(3):
            h, c = heads[r], slice(128 * r, 128 * r + 128)
            oT[h:h + 64, cols] = o[:, c]
            a, b = dq[0:32, c], dq[32:64, c]
            dqkvT[h:h + 32, cols] = (a * cos + b * sin).astype(BF)
            dqkvT[h + 32:h + 64, cols] = (b * cos - a * sin).astype(BF)
        dqkvT[768 + 64 * g:832 + 64 * g, cols] = nt(do3, pbd).astype(BF)
        dk = nt(q3, dsbd)
        a, b = dk[0:32], dk[32:64]
        dqkvT[576 + 64 * g:608 + 64 * g, cols] = (a * cos + b * sin).astype(BF)
        dqkvT[608 + 64 * g:640 + 64 * g, cols] = (b * cos - a * sin).astype(BF)


def attn_kernel(x, dy, w, tab, dx, dwq, dwk, dwv, dwo, qkvT, doT, kl, vl, oT, dqkvT):
    @pl.loop(0, 8)
    def _(i):
        project(i, w, x, dy, tab, qkvT, doT, kl, vl)

    @pl.loop(0, 16)
    def _(j):
        attend(j, tab, qkvT, doT, kl, vl, oT, dqkvT)

    @pl.loop(0, 8)
    def _(i):
        rows = pl.ds(pl.multiple_of(i * 256, 256), 256)
        dx[rows, :] = tn(dqkvT[:, rows], w[0:960, :]).astype(BF)

    for lo in (0, 288):
        dwq[lo:lo + 288] = nn(dqkvT[lo:lo + 288, :], x[...])
        dwo[lo:lo + 288] = nn(oT[lo:lo + 288, :], dy[...])
    dkv = nn(dqkvT[576:960, :], x[...])
    dwk[...] = dkv[0:192]
    dwv[...] = dkv[192:384]


def attn(x, dy, w, tab):
    vm = pl.BlockSpec(memory_space=pltpu.VMEM)
    return pl.pallas_call(
        attn_kernel,
        out_shape=(jax.ShapeDtypeStruct((T, D), BF), jax.ShapeDtypeStruct((576, D), F32), jax.ShapeDtypeStruct((192, D), F32),
                   jax.ShapeDtypeStruct((192, D), F32), jax.ShapeDtypeStruct((576, D), F32)),
        in_specs=[vm] * 4, out_specs=[vm] * 5,
        scratch_shapes=[pltpu.VMEM((960, T), BF), pltpu.VMEM((576, T), BF), pltpu.VMEM((3, 1024, 128), BF),
                        pltpu.VMEM((3, 1024, 128), BF), pltpu.VMEM((576, T), BF), pltpu.VMEM((960, T), BF)],
        compiler_params=pltpu.CompilerParams(vmem_limit_bytes=60 * 2**20),
        cost_estimate=pl.CostEstimate(flops=40_000_000_000, bytes_accessed=20_000_000, transcendentals=1_000_000),
        name="attn_backward",
    )(x, dy, w, tab)


def solution(mesh):
    fsdp = ("row", "col")
    every = ("dp", "row", "col")

    def step(x_loc, dy_loc, wq, wk, wv, wo, g):
        slab = jnp.concatenate([jnp.transpose(wq, (1, 2, 0)).reshape(576, 72), jnp.transpose(wk, (1, 2, 0)).reshape(192, 72),
                                jnp.transpose(wv, (1, 2, 0)).reshape(192, 72), wo.reshape(576, 72)], axis=0)
        w = lax.all_gather(slab, fsdp, axis=1, tiled=True)
        group_sum = lax.psum_scatter(g.astype(BF), fsdp, scatter_dimension=3, tiled=True)
        dw_next = lax.psum(group_sum.astype(F32), "dp")[0]
        dx, dwq, dwk, dwv, dwo = attn(x_loc.reshape(T, D), dy_loc.reshape(T, D), w, jnp.asarray(rope_tables()))

        def head_first(a, n):
            return jnp.transpose(a.reshape(n, 64, D), (2, 0, 1))[None]

        return (dx.reshape(32, 64, D), dw_next, head_first(dwq, 9), head_first(dwk, 3), head_first(dwv, 3),
                dwo.reshape(1, 9, 64, D))

    return jax.shard_map(
        step, mesh=mesh,
        in_specs=(P(every), P(every), P(fsdp), P(fsdp), P(fsdp), P(None, None, fsdp), P(every)),
        out_specs=(P(every), P(None, None, fsdp), P(every), P(every), P(every), P(every)),
        check_vma=False)
```

profile of v0, /device:TPU:0, one launch (start us, length us, event | category | flops | bytes accessed | tf_op | source)
XLA Modules:
  0.0 194.3 jit_solution(1280680612251134758)
XLA Ops:
  7.2 0.0 all-gather.2.cloned.1.call-start
  7.2 1.1 pad_maximum_fusion
  8.3 0.9 copy.27
  9.2 0.0 all-gather.2.cloned.1.call-update
  9.2 0.0 reduce-scatter.4.cloned.1.call-start
  9.3 7.0 %convert_element_type.6 = bf16[1,3,576,1536]{3,2,1,0:T(8,128)(2,1)} convert(f32[1,3,576,1536]{3,2,1,0:T(8,128)} %param.14) | non-fusion elementwise | flops 2654208 | bytes 15925248 | tf_op jit(solution)/shard_map/convert_element_type | solution.py:141
  16.3 12.5 %copy.30 = bf16[1,3,576,1536]{2,1,0,3:T(4,128)(2,1)} copy(bf16[1,3,576,1536]{3,2,1,0:T(8,128)(2,1)} %convert_element_type.6) | data formatting | bytes 10616832
  28.8 15.8 %reshape.56 = bf16[1536,1728]{1,0:T(8,128)(2,1)} reshape(bf16[1536,1,3,576]{3,2,1,0:T(4,128)(2,1)} %bitcast.34) | data formatting | bytes 10616832
  44.6 0.0 reduce-scatter.4.cloned.1.call-update
  44.6 0.0 all-reduce.2.cloned.1.call-start
  44.7 0.0 all-gather.2.cloned.1.call-done
  44.7 3.9 %copy.28.w = bf16[1536,576]{1,0:T(8,128)(2,1)} copy(bf16[1536,576]{0,1:T(8,128)(2,1)} %all-gather.2.cloned.1.call-done) | data formatting | bytes 3538944 | tf_op jit(solution)/shard_map/all_gather | solution.py:140
  48.6 56.1 %reduce-scatter.4.cloned.1.call-done = bf16[192,1728]{1,0:T(8,128)(2,1)} async-done(((bf16[1536,1728]{1,0:T(8,128)(2,1)}), bf16[192,1728]{1,0:T(8,128)(2,1)}) %reduce-scatter.4.cloned.1.call-update) | async-done | bytes 663568
  104.8 2.5 %reshape.57 = bf16[192,1,3,576]{3,2,1,0:T(4,128)(2,1)S(1)} reshape(bf16[192,1728]{1,0:T(8,128)(2,1)} %reduce-scatter.4.cloned.1.call-done) | data formatting | bytes 1327104
  107.2 1.3 copy.31
  108.5 1.4 bitcast_convert_fusion
  109.9 0.0 all-reduce.2.cloned.1.call-update
  109.9 39.0 %attn_backward.1 = (bf16[2048,576]{1,0:T(8,128)(2,1)}, f32[576,576]{1,0:T(8,128)}, f32[192,576]{1,0:T(8,128)}, f32[192,576]{1,0:T(8,128)}, f32[576,576]{1,0:T(8,128)}) custom-call(bf16[2048,576]{1,0:T(8,128)(2,1)} %bitcast.40, bf16[2048,576]{1,0:T(8,128)(2,1)} %bitcast.41, bf16[1536,576]{1,0:T(8,128)(2,1)} %copy.28.w, f32[2,32,256]{2,1,0:T(8,128)} %constant.2.clone.tab), custom_call_target="tpu_custom_call" | custom-call | flops 40000000000 | bytes 20000000 | tf_op jit(solution)/shard_map/attn_backward/pallas_call | solution.py:120
  148.9 36.2 %all-reduce.2.cloned.1.call-done = f32[3,576,192]{2,1,0:T(8,128)} async-done(((f32[3,576,192]{2,1,0:T(8,128)}), f32[3,576,192]{2,1,0:T(8,128)}) %all-reduce.2.cloned.1.call-update) | async-done | bytes 1327120 | tf_op jit(solution)/shard_map/psum | solution.py:142
  185.1 2.6 %copy.29 = f32[3,576,192]{1,2,0:T(8,128)} copy(f32[3,576,192]{2,1,0:T(8,128)} %all-reduce.2.cloned.1.call-done) | data formatting | bytes 2654208
Async XLA Ops:
  7.2 37.5 %all-gather.2.cloned.1.call-start = ((), (), s32[]{:S(2)}) async-start(), calls=%async_computation.1 | async-start | bytes 1990656 | tf_op jit(solution)/shard_map/all_gather | solution.py:140
  9.2 95.6 %reduce-scatter.4.cloned.1.call-start = ((), (), s32[]{:S(2)}) async-start(), calls=%async_computation.3 | async-start | bytes 6193152
  44.6 140.5 %all-reduce.2.cloned.1.call-start = ((), (), s32[]{:S(2)}) async-start(), calls=%async_computation.2 | async-start | bytes 3538944 | tf_op jit(solution)/shard_map/psum | solution.py:142
Sparse Core Ops, SparseCore 0:
  10.4 28.8 all-gather.1
  44.8 59.9 reduce-scatter.3
  110.0 75.0 all-reduce.1
where the time goes:
time: 195 us; the launch traced here: 194 us
  waiting for transfers between devices  92.5 us (47%)
  local copies, waits for them, and re-layouts  39.4 us (20%)
  Pallas kernels  39 us (20%)
  between operations  13.8 us (7%)
  other arithmetic  9.5 us (5%)
    unnamed x4, waiting for transfers between devices  56.2 us
    pallas_call x1, Pallas kernels, attn(): pl.pallas_call(attn_kernel, out_shape=(jax.ShapeDtypeStruct((T, D), BF),...  39 us
    psum x1, waiting for transfers between devices, step(): dw_next = lax.psum(group_sum.astype(F32), 'dp')[0]  36.2 us
    unnamed x5, local copies, waits for them, and re-layouts  34.7 us
    convert_element_type x1, other arithmetic, step(): g.astype(BF)  7.03 us
    all_gather x1, local copies, waits for them, and re-layouts, step(): w = lax.all_gather(slab, fsdp, axis=1, tiled=True)  3.9 us
  transfers between devices with their start and end apart: 3, of which 2 were waited for; matrix products, arithmetic and copies ran while one was open for 20% of the time, Pallas kernels for 20%

commit v1 on v0

--- a/solution.py
+++ b/solution.py
@@ -93,41 +93,318 @@
         dqkvT[608 + 64 * g:640 + 64 * g, cols] = (b * cos - a * sin).astype(BF)
 
 
-def attn_kernel(x, dy, w, tab, dx, dwq, dwk, dwv, dwo, qkvT, doT, kl, vl, oT, dqkvT):
+NP = 18
+MESH = pl.DeviceIdType.MESH
+
+
+def flip(bit, other):
+    return 1 - other if bit else other
+
+
+class Comm:
+    def __init__(self, g, out, wl, pk, gf, gsh, d2d, u, r1, v, r2, gs, ze, za, zr, zf, outs, ssem, rsem, wss, wsr, gsem, osem):
+        self.__dict__.update({k: val for k, val in locals().items() if k != "self"})
+        self.z, self.y, self.col = lax.axis_index("dp"), lax.axis_index("row"), lax.axis_index("col")
+        self.c, self.x = lax.rem(self.col, 2), lax.div(self.col, 2)
+        self.sib = self.col + 1 - 2 * self.c
+        self.xcol = (1 - self.x) * 2 + self.c
+        self.yrow = 1 - self.y
+        self.zp = self.z + 1 - 2 * lax.rem(self.z, 2)
+        self.zm = 3 - self.z
+        self.mid = (self.z == 1) | (self.z == 2)
+        self.end = (self.z == 0) | (self.z == 3)
+        self.sibling, self.xdev = (self.z, self.y, self.sib), (self.z, self.y, self.xcol)
+        self.ydev, self.zdev, self.mdev = (self.z, self.yrow, self.col), (self.zp, self.y, self.col), (self.zm, self.y, self.col)
+
+    def barrier(self):
+        sem = pltpu.get_barrier_semaphore()
+        for dev in (self.sibling, self.xdev, self.ydev, self.zdev):
+            pl.semaphore_signal(sem, inc=1, device_id=dev, device_id_type=MESH)
+
+        @pl.when(self.mid)
+        def _():
+            pl.semaphore_signal(sem, inc=1, device_id=self.mdev, device_id_type=MESH)
+
+        pl.semaphore_wait(sem, 4 + lax.rem(lax.div(self.z + 1, 2), 2))
+
+    def pack(self):
+        mine = 4 * self.y + self.col
+        self.pk[mine] = jnp.concatenate([self.wl[96 * j:96 * j + 96, :] for j in range(16)], axis=1)
+
+    def unpack(self, w):
+        for j in range(16):
+            w[96 * j:96 * j + 96, :] = jnp.concatenate([self.pk[i, :, 72 * j:72 * j + 72] for i in range(8)], axis=1)
+
+    def wcopy(self, n):
+        me = 4 * self.y + self.col
+        fx, fy, fd = 4 * self.y + self.xcol, 4 * self.yrow + self.col, 4 * self.yrow + self.xcol
+        slab, lo, size, dev = (
+            (me, 0, 48, self.xdev), (me, 48, 48, self.ydev), (me, 48, 48, self.xdev), (me, 0, 48, self.ydev),
+            (me, 0, 96, self.sibling),
+            (fx, 0, 48, self.ydev), (fy, 48, 48, self.xdev),
+            (fx, 0, 96, self.sibling), (fy, 0, 96, self.sibling),
+            (fd, 0, 48, self.sibling), (fd, 48, 48, self.sibling))[n]
+        ref = self.pk.at[slab, pl.ds(lo, size), :]
+        return pltpu.make_async_remote_copy(ref, ref, self.wss.at[n], self.wsr.at[n], device_id=dev, device_id_type=MESH)
+
+    def load(self, p):
+        k, r, slot = lax.div(p, 6), lax.rem(p, 6), lax.rem(p, 4)
+        return [pltpu.make_async_copy(self.g.at[k, pl.ds(pl.multiple_of(288 * h + 48 * r, 48), 48), :],
+                                      self.gf.at[slot, pl.ds(48 * h, 48), :], self.gsem.at[h, p]) for h in range(2)]
+
+    def remote(self, n, src, dst, p, dev):
+        return pltpu.make_async_remote_copy(src, dst, self.ssem.at[n, p], self.rsem.at[n, p], device_id=dev, device_id_type=MESH)
+
+    def c0(self, p):
+        return self.remote(0, self.gsh.at[p, 1], self.d2d.at[p], p, self.sibling)
+
+    def c1(self, p):
+        t = lax.rem(p, 2)
+        dev = (self.z, self.y + t * (self.yrow - self.y), self.xcol + t * (self.col - self.xcol))
+        return self.remote(1, self.u.at[p, 1], self.r1.at[p], p, dev)
+
+    def c2(self, p):
+        t = lax.rem(p, 2)
+        dev = (self.z, self.yrow + t * (self.y - self.yrow), self.col + t * (self.xcol - self.col))
+        return self.remote(2, self.v.at[p, 1], self.r2.at[p], p, dev)
+
+    def c3(self, p):
+        return self.remote(3, self.gs.at[p], self.ze.at[p], p, self.zdev)
+
+    def c4(self, p):
+        return self.remote(4, self.za.at[p], self.zr.at[p], p, self.mdev)
+
+    def c5(self, p):
+        return self.remote(5, self.zf.at[p], self.zr.at[p], p, self.zdev)
+
+    def s1(self, p):
+        for cp in self.load(p):
+            cp.wait()
+        slot = lax.rem(p, 4)
+        for q in range(4):
+            top = self.gf[slot, 0:48, 384 * q:384 * q + 384].astype(BF)
+            bot = self.gf[slot, 48:96, 384 * q:384 * q + 384].astype(BF)
+            for cc in range(2):
+                lanes = slice(192 * cc, 192 * cc + 192)
+                self.gsh[p, flip(cc, self.c), q] = jnp.concatenate([top[:, lanes], bot[:, lanes]], axis=1)
+        self.c0(p).start()
+
+        @pl.when(p + 4 < NP)
+        def _():
+            for cp in self.load(p + 4):
+                cp.start()
+
+    def s2(self, p):
+        self.c0(p).wait_recv()
+        t = lax.rem(p, 2)
+        for yy in range(2):
+            for xx in range(2):
+                q = 2 * yy + xx
+                fx, fy = flip(xx, self.x), flip(yy, self.y)
+                self.u[p, fx + t * (fy - fx), yy + t * (xx - yy)] = self.gsh[p, 0, q] + self.d2d[p, q]
+        self.c1(p).start()
+
+    def s3(self, p):
+        self.c1(p).wait_recv()
+        t = lax.rem(p, 2)
+        own = self.y + t * (self.x - self.y)
+        for e in range(2):
+            self.v[p, flip(e, own)] = self.u[p, 0, e] + self.r1[p, e]
+        self.c2(p).start()
+
+    def s4(self, p):
+        self.c2(p).wait_recv()
+        self.gs[p] = self.v[p, 0] + self.r2[p]
+
+        @pl.when(self.end)
+        def _():
+            self.c3(p).start()
+
+    def s5(self, p):
+        @pl.when(self.mid)
+        def _():
+            self.c3(p).wait_recv()
+            self.za[p] = self.gs[p].astype(F32) + self.ze[p].astype(F32)
+            self.c4(p).start()
+
+    def s6(self, p):
+        @pl.when(self.mid)
+        def _():
+            self.c4(p).wait_recv()
+            self.zf[p] = self.za[p] + self.zr[p]
+            self.c5(p).start()
+
+            @pl.when(lax.rem(p, 6) == 5)
+            def _():
+                self.emit(self.zf, lax.div(p, 6))
+
+    def s7(self, p):
+        @pl.when(self.end)
+        def _():
+            self.c5(p).wait_recv()
+
+            @pl.when(lax.rem(p, 6) == 5)
+            def _():
+                self.emit(self.zr, lax.div(p, 6))
+
+    def emit(self, buf, k):
+        tr = buf[pl.ds(6 * k, 6)].reshape(288, 384).T
+        self.outs[k] = jnp.concatenate([tr[0:192], tr[192:384]], axis=1)
+        self.ocopy(k).start()
+
+    def ocopy(self, k):
+        return pltpu.make_async_copy(self.outs.at[k], self.out.at[k], self.osem.at[k])
+
+    def step(self, t):
+        for off, stage in zip(OFFSETS, (self.s1, self.s2, self.s3, self.s4, self.s5, self.s6, self.s7)):
+            p = t - off
+
+            @pl.when((p >= 0) & (p < NP))
+            def _():
+                stage(p)
+
+    def drain(self):
+        for n in range(11):
+            self.wcopy(n).wait_send()
+
+        @pl.loop(0, NP)
+        def _(p):
+            self.c0(p).wait_send()
+            self.c1(p).wait_send()
+            self.c2(p).wait_send()
+
+            @pl.when(self.end)
+            def _():
+                self.c3(p).wait_send()
+
+            @pl.when(self.mid)
+            def _():
+                self.c4(p).wait_send()
+                self.c5(p).wait_send()
+
+        for k in range(3):
+            self.ocopy(k).wait()
+
+
+OFFSETS = (0, 1, 3, 5, 6, 8, 10)
+
+
+def kernel(x_h, dy_h, wq_h, wk_h, wv_h, wo_h, g, tab, dx_h, dwq_h, dwk_h, dwv_h, dwo_h, out,
+           x, dy, w, qkvT, doT, kl, vl, oT, dqkvT, dx, dws, insem, outsem, *bufs):
+    cm = Comm(g, out, *bufs)
+    loads = [pltpu.make_async_copy(src, cm.wl.at[lo:lo + n, :], insem.at[i])
+             for i, (src, lo, n) in enumerate(((wq_h, 0, 576), (wk_h, 576, 192), (wv_h, 768, 192), (wo_h, 960, 576)))]
+    for cp in loads:
+        cp.start()
+    for p in range(4):
+        for cp in cm.load(p):
+            cp.start()
+    acts = [pltpu.make_async_copy(x_h, x, insem.at[4]), pltpu.make_async_copy(dy_h, dy, insem.at[5])]
+    for cp in acts:
+        cp.start()
+    cm.barrier()
+    for cp in loads:
+        cp.wait()
+    cm.pack()
+    for n in range(5):
+        cm.wcopy(n).start()
+    cm.step(0)
+    cm.wcopy(0).wait_recv()
+    cm.wcopy(5).start()
+    cm.wcopy(1).wait_recv()
+    cm.wcopy(6).start()
+    cm.step(1)
+    cm.wcopy(2).wait_recv()
+    cm.wcopy(7).start()
+    cm.wcopy(3).wait_recv()
+    cm.wcopy(8).start()
+    cm.step(2)
+    cm.wcopy(5).wait_recv()
+    cm.wcopy(9).start()
+    cm.wcopy(6).wait_recv()
+    cm.wcopy(10).start()
+    for n in (4, 7, 8, 9, 10):
+        cm.wcopy(n).wait_recv()
+    cm.unpack(w)
+    for cp in acts:
+        cp.wait()
+
     @pl.loop(0, 8)
     def _(i):
         project(i, w, x, dy, tab, qkvT, doT, kl, vl)
 
+        @pl.when(lax.rem(i, 2) == 1)
+        def _():
+            cm.step(3 + lax.div(i, 2))
+
     @pl.loop(0, 16)
     def _(j):
         attend(j, tab, qkvT, doT, kl, vl, oT, dqkvT)
+        cm.step(7 + j)
+
+    def dx_copy(i):
+        rows = pl.ds(pl.multiple_of(i * 256, 256), 256)
+        return pltpu.make_async_copy(dx.at[rows, :], dx_h.at[rows, :], outsem.at[i])
 
     @pl.loop(0, 8)
     def _(i):
         rows = pl.ds(pl.multiple_of(i * 256, 256), 256)
         dx[rows, :] = tn(dqkvT[:, rows], w[0:960, :]).astype(BF)
-
-    for lo in (0, 288):
-        dwq[lo:lo + 288] = nn(dqkvT[lo:lo + 288, :], x[...])
-        dwo[lo:lo + 288] = nn(oT[lo:lo + 288, :], dy[...])
-    dkv = nn(dqkvT[576:960, :], x[...])
-    dwk[...] = dkv[0:192]
-    dwv[...] = dkv[192:384]
-
-
-def attn(x, dy, w, tab):
-    vm = pl.BlockSpec(memory_space=pltpu.VMEM)
+        dx_copy(i).start()
+
+        @pl.when(lax.rem(i, 2) == 1)
+        def _():
+            cm.step(23 + lax.div(i, 2))
+
+    def dw_copy(n):
+        src, dst = ((dws.at[0:288], dwq_h.at[0:288]), (dws.at[288:576], dwq_h.at[288:576]), (dws.at[960:1248], dwo_h.at[0:288]),
+                    (dws.at[1248:1536], dwo_h.at[288:576]), (dws.at[576:768], dwk_h), (dws.at[768:960], dwv_h))[n]
+        return pltpu.make_async_copy(src, dst, outsem.at[8 + n])
+
+    for h in range(2):
+        lo = 288 * h
+        dws[lo:lo + 288] = nn(dqkvT[lo:lo + 288, :], x[...])
+        dw_copy(h).start()
+        dws[960 + lo:1248 + lo] = nn(oT[lo:lo + 288, :], dy[...])
+        dw_copy(2 + h).start()
+    dws[576:960] = nn(dqkvT[576:960, :], x[...])
+    dw_copy(4).start()
+    dw_copy(5).start()
+
+    @pl.loop(27, NP + OFFSETS[-1])
+    def _(t):
+        cm.step(t)
+
+    for i in range(8):
+        dx_copy(i).wait()
+    for n in range(6):
+        dw_copy(n).wait()
+    cm.drain()
+
+
+def backward(x, dy, wq, wk, wv, wo, g, tab):
+    anyspace, vm = pl.BlockSpec(memory_space=pl.ANY), pl.BlockSpec(memory_space=pltpu.VMEM)
+
+    def buf(*shape, dtype=BF):
+        return pltpu.VMEM(shape, dtype)
+
+    dma = pltpu.SemaphoreType.DMA
     return pl.pallas_call(
-        attn_kernel,
+        kernel,
         out_shape=(jax.ShapeDtypeStruct((T, D), BF), jax.ShapeDtypeStruct((576, D), F32), jax.ShapeDtypeStruct((192, D), F32),
-                   jax.ShapeDtypeStruct((192, D), F32), jax.ShapeDtypeStruct((576, D), F32)),
-        in_specs=[vm] * 4, out_specs=[vm] * 5,
-        scratch_shapes=[pltpu.VMEM((960, T), BF), pltpu.VMEM((576, T), BF), pltpu.VMEM((3, 1024, 128), BF),
-                        pltpu.VMEM((3, 1024, 128), BF), pltpu.VMEM((576, T), BF), pltpu.VMEM((960, T), BF)],
-        compiler_params=pltpu.CompilerParams(vmem_limit_bytes=60 * 2**20),
-        cost_estimate=pl.CostEstimate(flops=40_000_000_000, bytes_accessed=20_000_000, transcendentals=1_000_000),
-        name="attn_backward",
-    )(x, dy, w, tab)
+                   jax.ShapeDtypeStruct((192, D), F32), jax.ShapeDtypeStruct((576, D), F32),
+                   jax.ShapeDtypeStruct((3, 192, D), F32)),
+        in_specs=[anyspace] * 7 + [vm], out_specs=[anyspace] * 6,
+        scratch_shapes=[
+            buf(T, D), buf(T, D), buf(1536, D), buf(960, T), buf(576, T), buf(3, 1024, 128), buf(3, 1024, 128), buf(576, T),
+            buf(960, T), buf(T, D), buf(1536, D, dtype=F32), dma((6,)), dma((14,)),
+            buf(1536, 72), buf(8, 96, 1152), buf(4, 96, 1536, dtype=F32), buf(NP, 2, 4, 48, 384), buf(NP, 4, 48, 384),
+            buf(NP, 2, 2, 48, 384), buf(NP, 2, 48, 384), buf(NP, 2, 48, 384), buf(NP, 48, 384), buf(NP, 48, 384),
+            buf(NP, 48, 384), buf(NP, 48, 384, dtype=F32), buf(NP, 48, 384, dtype=F32), buf(NP, 48, 384, dtype=F32),
+            buf(3, 192, D, dtype=F32), dma((6, NP)), dma((6, NP)), dma((11,)), dma((11,)), dma((2, NP)), dma((3,))],
+        compiler_params=pltpu.CompilerParams(vmem_limit_bytes=67_000_000, collective_id=0, has_side_effects=True),
+        name="attn_backward_and_sum",
+    )(x, dy, wq, wk, wv, wo, g, tab)
 
 
 def solution(mesh):
@@ -135,18 +412,18 @@
     every = ("dp", "row", "col")
 
     def step(x_loc, dy_loc, wq, wk, wv, wo, g):
-        slab = jnp.concatenate([jnp.transpose(wq, (1, 2, 0)).reshape(576, 72), jnp.transpose(wk, (1, 2, 0)).reshape(192, 72),
-                                jnp.transpose(wv, (1, 2, 0)).reshape(192, 72), wo.reshape(576, 72)], axis=0)
-        w = lax.all_gather(slab, fsdp, axis=1, tiled=True)
-        group_sum = lax.psum_scatter(g.astype(BF), fsdp, scatter_dimension=3, tiled=True)
-        dw_next = lax.psum(group_sum.astype(F32), "dp")[0]
-        dx, dwq, dwk, dwv, dwo = attn(x_loc.reshape(T, D), dy_loc.reshape(T, D), w, jnp.asarray(rope_tables()))
+        def rows_first(a):
+            return jnp.transpose(a, (1, 2, 0)).reshape(-1, 72)
+
+        dx, dwq, dwk, dwv, dwo, dw_next = backward(
+            x_loc.reshape(T, D), dy_loc.reshape(T, D), rows_first(wq), rows_first(wk), rows_first(wv), wo.reshape(576, 72),
+            g[0], jnp.asarray(rope_tables()))
 
         def head_first(a, n):
             return jnp.transpose(a.reshape(n, 64, D), (2, 0, 1))[None]
 
-        return (dx.reshape(32, 64, D), dw_next, head_first(dwq, 9), head_first(dwk, 3), head_first(dwv, 3),
-                dwo.reshape(1, 9, 64, D))
+        return (dx.reshape(32, 64, D), jnp.transpose(dw_next, (0, 2, 1)), head_first(dwq, 9), head_first(dwk, 3),
+                head_first(dwv, 3), dwo.reshape(1, 9, 64, D))
 
     return jax.shard_map(
         step, mesh=mesh,

time: 195 us -> 85.6 us (0.44)
  waiting for transfers between devices: 92.5 us -> 0 us
  Pallas kernels: 39 us -> 75.2 us
  local copies, waits for them, and re-layouts: 39.4 us -> 9.51 us
  between operations: 13.8 us -> 0.66 us
  other arithmetic: 9.5 us -> 0 us
    unnamed x4 -> x0, waiting for transfers between devices: 56.2 us -> none
    pallas_call x1, Pallas kernels: 39 us -> 75.2 us  [backward(): pl.pallas_call(kernel, out_shape=(jax.ShapeDtypeStruct((T, D), BF), jax.S...]
    psum x1 -> x0, waiting for transfers between devices: 36.2 us -> none  [step(): dw_next = lax.psum(group_sum.astype(F32), 'dp')[0]]
    unnamed x5 -> x16, local copies, waits for them, and re-layouts: 34.7 us -> 9.51 us
    convert_element_type x1 -> x0, other arithmetic: 7.03 us -> none  [step(): g.astype(BF)]
    all_gather x1 -> x0, local copies, waits for them, and re-layouts: 3.9 us -> none  [step(): w = lax.all_gather(slab, fsdp, axis=1, tiled=True)]
  transfers between devices with their start and end apart: 3 -> 0, of which waited for: 2 -> 0; matrix products, arithmetic and copies ran while one was open for 20% -> 0% of each run, Pallas kernels for 20% -> 0%
where the time goes in v1:
time: 85.6 us; the launch traced here: 85.4 us
  Pallas kernels  75.2 us (88%)
  local copies, waits for them, and re-layouts  9.51 us (11%)
    pallas_call x1, Pallas kernels, backward(): pl.pallas_call(kernel, out_shape=(jax.ShapeDtypeStruct((T, D), BF), jax.S...  75.2 us
    unnamed x16, local copies, waits for them, and re-layouts  9.51 us

profile of v1, /device:TPU:0, one launch (start us, length us, event | category | flops | bytes accessed | tf_op | source)
XLA Modules:
  0.0 85.4 jit_solution(11281698881835671683)
XLA Ops:
  0.6 75.2 %attn_backward_and_sum.1 = (bf16[2048,576]{1,0:T(8,128)(2,1)}, f32[576,576]{1,0:T(8,128)}, f32[192,576]{1,0:T(8,128)}, f32[192,576]{1,0:T(8,128)}, f32[576,576]{1,0:T(8,128)}, /*index=5*/f32[3,192,576]{2,1,0:T(8,128)}) custom-call(bf16[2048,576]{1,0:T(8,128)(2,1)} %bitcast.32, bf16[2048,576]{1,0:T(8,128)(2,1)} %bitcast.33, bf16[576,72]{1,0:T(8,128)(2,1)} %bitcast.40, ...), custom_call_target="tpu_custom_call" | custom-call | tf_op jit(solution)/shard_map/attn_backward_and_sum/pallas_call | solution.py:392
  75.9 0.0 copy-start.2
  75.9 3.6 %copy.20 = bf16[32,64,576]{2,1,0:T(8,128)(2,1)} copy(bf16[32,64,576]{2,1,0:T(8,128)(2,1)} %bitcast.34) | data formatting | bytes 4718592
  79.4 0.0 copy-done.2
  79.4 0.0 copy-start.1
  79.4 1.1 %copy.21 = f32[3,576,192]{1,2,0:T(8,128)} copy(f32[3,576,192]{1,2,0:T(8,128)S(1)} %bitcast.37) | data formatting | bytes 2654208
  80.6 0.8 copy-done.1
  81.3 0.0 copy-start.4
  81.3 0.0 copy-start.3
  81.4 1.1 %copy.22 = f32[1,576,9,64]{1,3,2,0:T(8,128)} copy(f32[1,576,9,64]{1,3,2,0:T(8,128)S(1)} %bitcast.36) | data formatting | bytes 2654208
  82.5 0.2 copy-done.4
  82.7 0.0 copy-start
  82.7 0.8 copy.23
  83.5 0.0 copy-done.3
  83.5 0.8 copy.24
  84.2 0.0 copy-done
  84.3 1.1 %copy.25 = f32[1,9,64,576]{3,2,1,0:T(8,128)} copy(f32[1,9,64,576]{3,2,1,0:T(8,128)S(1)} %bitcast.35) | data formatting | bytes 2654208
Async XLA Ops:
  75.9 3.6 %copy-start.2 = (f32[3,192,576]{2,1,0:T(8,128)S(1)}, f32[3,192,576]{2,1,0:T(8,128)}, u32[]{:S(2)}) copy-start(f32[3,192,576]{2,1,0:T(8,128)} %get-tuple-element.13) | copy-start | bytes 3981316
  79.4 1.9 %copy-start.1 = (f32[576,576]{1,0:T(8,128)S(1)}, f32[576,576]{1,0:T(8,128)}, u32[]{:S(2)}) copy-start(f32[576,576]{1,0:T(8,128)} %get-tuple-element.14) | copy-start | bytes 3981316
  81.3 1.3 %copy-start.4 = (f32[192,576]{1,0:T(8,128)S(1)}, f32[192,576]{1,0:T(8,128)}, u32[]{:S(2)}) copy-start(f32[192,576]{1,0:T(8,128)} %get-tuple-element.15) | copy-start | bytes 1327108
  81.3 2.1 %copy-start.3 = (f32[192,576]{1,0:T(8,128)S(1)}, f32[192,576]{1,0:T(8,128)}, u32[]{:S(2)}) copy-start(f32[192,576]{1,0:T(8,128)} %get-tuple-element.16) | copy-start | bytes 1327108
  82.7 1.6 %copy-start = (f32[576,576]{1,0:T(8,128)S(1)}, f32[576,576]{1,0:T(8,128)}, u32[]{:S(2)}) copy-start(f32[576,576]{1,0:T(8,128)} %get-tuple-element.17) | copy-start | bytes 3981316

commit v2 on v1

--- a/solution.py
+++ b/solution.py
@@ -102,7 +102,7 @@
 
 
 class Comm:
-    def __init__(self, g, out, wl, pk, gf, gsh, d2d, u, r1, v, r2, gs, ze, za, zr, zf, outs, ssem, rsem, wss, wsr, gsem, osem):
+    def __init__(self, g, out, wl, pk, gf, gsh, d2d, u, r1, v, r2, gs, ze, za, zr, zf, ssem, rsem, wss, wsr, gsem):
         self.__dict__.update({k: val for k, val in locals().items() if k != "self"})
         self.z, self.y, self.col = lax.axis_index("dp"), lax.axis_index("row"), lax.axis_index("col")
         self.c, self.x = lax.rem(self.col, 2), lax.div(self.col, 2)
@@ -194,6 +194,15 @@
             for cp in self.load(p + 4):
                 cp.start()
 
+    def convert(self, lo, hi):
+        @pl.loop(lo, hi)
+        def _(p):
+            self.s1(p)
+
+    def forward(self, got, send):
+        self.wcopy(got).wait_recv()
+        self.wcopy(send).start()
+
     def s2(self, p):
         self.c0(p).wait_recv()
         t = lax.rem(p, 2)
@@ -249,14 +258,10 @@
 
     def emit(self, buf, k):
         tr = buf[pl.ds(6 * k, 6)].reshape(288, 384).T
-        self.outs[k] = jnp.concatenate([tr[0:192], tr[192:384]], axis=1)
-        self.ocopy(k).start()
-
-    def ocopy(self, k):
-        return pltpu.make_async_copy(self.outs.at[k], self.out.at[k], self.osem.at[k])
+        self.out[k] = jnp.concatenate([tr[0:192], tr[192:384]], axis=1)
 
     def step(self, t):
-        for off, stage in zip(OFFSETS, (self.s1, self.s2, self.s3, self.s4, self.s5, self.s6, self.s7)):
+        for off, stage in zip(OFFSETS, (self.s2, self.s3, self.s4, self.s5, self.s6, self.s7)):
             p = t - off
 
             @pl.when((p >= 0) & (p < NP))
@@ -282,15 +287,12 @@
                 self.c4(p).wait_send()
                 self.c5(p).wait_send()
 
-        for k in range(3):
-            self.ocopy(k).wait()
-
-
-OFFSETS = (0, 1, 3, 5, 6, 8, 10)
-
-
-def kernel(x_h, dy_h, wq_h, wk_h, wv_h, wo_h, g, tab, dx_h, dwq_h, dwk_h, dwv_h, dwo_h, out,
-           x, dy, w, qkvT, doT, kl, vl, oT, dqkvT, dx, dws, insem, outsem, *bufs):
+
+OFFSETS = (0, 3, 5, 7, 10, 13)
+
+
+def kernel(x_h, dy_h, wq_h, wk_h, wv_h, wo_h, g, tab, dx, dwq, dwk, dwv, dwo, out,
+           x, dy, w, qkvT, doT, kl, vl, oT, dqkvT, insem, *bufs):
     cm = Comm(g, out, *bufs)
     loads = [pltpu.make_async_copy(src, cm.wl.at[lo:lo + n, :], insem.at[i])
              for i, (src, lo, n) in enumerate(((wq_h, 0, 576), (wk_h, 576, 192), (wv_h, 768, 192), (wo_h, 960, 576)))]
@@ -308,82 +310,70 @@
     cm.pack()
     for n in range(5):
         cm.wcopy(n).start()
+    cm.convert(0, 3)
     cm.step(0)
-    cm.wcopy(0).wait_recv()
-    cm.wcopy(5).start()
-    cm.wcopy(1).wait_recv()
-    cm.wcopy(6).start()
+    cm.convert(3, 5)
     cm.step(1)
-    cm.wcopy(2).wait_recv()
-    cm.wcopy(7).start()
-    cm.wcopy(3).wait_recv()
-    cm.wcopy(8).start()
+    cm.forward(0, 5)
+    cm.forward(1, 6)
+    cm.convert(5, 9)
     cm.step(2)
-    cm.wcopy(5).wait_recv()
-    cm.wcopy(9).start()
-    cm.wcopy(6).wait_recv()
-    cm.wcopy(10).start()
+    cm.forward(2, 7)
+    cm.forward(3, 8)
+    cm.convert(9, 13)
+    cm.step(3)
+    cm.convert(13, NP)
+    cm.step(4)
+    cm.forward(5, 9)
+    cm.forward(6, 10)
+    cm.step(5)
     for n in (4, 7, 8, 9, 10):
         cm.wcopy(n).wait_recv()
     cm.unpack(w)
     for cp in acts:
         cp.wait()
 
+    def some(i, first, period, of):
+        @pl.when(lax.rem(i, period) < of)
+        def _():
+            cm.step(first + of * lax.div(i, period) + lax.rem(i, period))
+
     @pl.loop(0, 8)
     def _(i):
         project(i, w, x, dy, tab, qkvT, doT, kl, vl)
-
-        @pl.when(lax.rem(i, 2) == 1)
-        def _():
-            cm.step(3 + lax.div(i, 2))
+        some(i, 6, 3, 2)
 
     @pl.loop(0, 16)
     def _(j):
         attend(j, tab, qkvT, doT, kl, vl, oT, dqkvT)
-        cm.step(7 + j)
-
-    def dx_copy(i):
-        rows = pl.ds(pl.multiple_of(i * 256, 256), 256)
-        return pltpu.make_async_copy(dx.at[rows, :], dx_h.at[rows, :], outsem.at[i])
+        some(j, 12, 3, 2)
 
     @pl.loop(0, 8)
     def _(i):
         rows = pl.ds(pl.multiple_of(i * 256, 256), 256)
         dx[rows, :] = tn(dqkvT[:, rows], w[0:960, :]).astype(BF)
-        dx_copy(i).start()
-
-        @pl.when(lax.rem(i, 2) == 1)
-        def _():
-            cm.step(23 + lax.div(i, 2))
-
-    def dw_copy(n):
-        src, dst = ((dws.at[0:288], dwq_h.at[0:288]), (dws.at[288:576], dwq_h.at[288:576]), (dws.at[960:1248], dwo_h.at[0:288]),
-                    (dws.at[1248:1536], dwo_h.at[288:576]), (dws.at[576:768], dwk_h), (dws.at[768:960], dwv_h))[n]
-        return pltpu.make_async_copy(src, dst, outsem.at[8 + n])
-
-    for h in range(2):
-        lo = 288 * h
-        dws[lo:lo + 288] = nn(dqkvT[lo:lo + 288, :], x[...])
-        dw_copy(h).start()
-        dws[960 + lo:1248 + lo] = nn(oT[lo:lo + 288, :], dy[...])
-        dw_copy(2 + h).start()
-    dws[576:960] = nn(dqkvT[576:960, :], x[...])
-    dw_copy(4).start()
-    dw_copy(5).start()
-
-    @pl.loop(27, NP + OFFSETS[-1])
+        some(i, 23, 2, 1)
+
+    @pl.loop(0, 2)
+    def _(h):
+        rows = pl.ds(pl.multiple_of(288 * h, 288), 288)
+        dwq[rows, :] = nn(dqkvT[rows, :], x[...])
+        dwo[rows, :] = nn(oT[rows, :], dy[...])
+        cm.step(27 + h)
+
+    dkv = nn(dqkvT[576:960, :], x[...])
+    dwk[...] = dkv[0:192]
+    dwv[...] = dkv[192:384]
+
+    @pl.loop(29, NP + OFFSETS[-1])
     def _(t):
         cm.step(t)
 
-    for i in range(8):
-        dx_copy(i).wait()
-    for n in range(6):
-        dw_copy(n).wait()
     cm.drain()
 
 
 def backward(x, dy, wq, wk, wv, wo, g, tab):
-    anyspace, vm = pl.BlockSpec(memory_space=pl.ANY), pl.BlockSpec(memory_space=pltpu.VMEM)
+    hbm, vm = pl.BlockSpec(memory_space=pltpu.HBM), pl.BlockSpec(memory_space=pltpu.VMEM)
 
     def buf(*shape, dtype=BF):
         return pltpu.VMEM(shape, dtype)
@@ -391,20 +381,38 @@
     dma = pltpu.SemaphoreType.DMA
     return pl.pallas_call(
         kernel,
-        out_shape=(jax.ShapeDtypeStruct((T, D), BF), jax.ShapeDtypeStruct((576, D), F32), jax.ShapeDtypeStruct((192, D), F32),
-                   jax.ShapeDtypeStruct((192, D), F32), jax.ShapeDtypeStruct((576, D), F32),
-                   jax.ShapeDtypeStruct((3, 192, D), F32)),
-        in_specs=[anyspace] * 7 + [vm], out_specs=[anyspace] * 6,
+        out_shape=(buf(T, D), buf(576, D, dtype=F32), buf(192, D, dtype=F32), buf(192, D, dtype=F32), buf(576, D, dtype=F32),
+                   buf(3, 192, D, dtype=F32)),
+        in_specs=[hbm] * 7 + [vm], out_specs=[vm] * 6,
         scratch_shapes=[
             buf(T, D), buf(T, D), buf(1536, D), buf(960, T), buf(576, T), buf(3, 1024, 128), buf(3, 1024, 128), buf(576, T),
-            buf(960, T), buf(T, D), buf(1536, D, dtype=F32), dma((6,)), dma((14,)),
+            buf(960, T), dma((6,)),
             buf(1536, 72), buf(8, 96, 1152), buf(4, 96, 1536, dtype=F32), buf(NP, 2, 4, 48, 384), buf(NP, 4, 48, 384),
             buf(NP, 2, 2, 48, 384), buf(NP, 2, 48, 384), buf(NP, 2, 48, 384), buf(NP, 48, 384), buf(NP, 48, 384),
             buf(NP, 48, 384), buf(NP, 48, 384, dtype=F32), buf(NP, 48, 384, dtype=F32), buf(NP, 48, 384, dtype=F32),
-            buf(3, 192, D, dtype=F32), dma((6, NP)), dma((6, NP)), dma((11,)), dma((11,)), dma((2, NP)), dma((3,))],
-        compiler_params=pltpu.CompilerParams(vmem_limit_bytes=67_000_000, collective_id=0, has_side_effects=True),
+            dma((6, NP)), dma((6, NP)), dma((11,)), dma((11,)), dma((2, NP))],
+        compiler_params=pltpu.CompilerParams(vmem_limit_bytes=50 * 2**20, collective_id=0, has_side_effects=True),
         name="attn_backward_and_sum",
     )(x, dy, wq, wk, wv, wo, g, tab)
+
+
+def write_kernel(*refs):
+    n = len(refs) // 2
+    sem = refs[-1]
+    copies = [pltpu.make_async_copy(refs[i], refs[n + i], sem.at[i]) for i in range(n)]
+    for cp in copies:
+        cp.start()
+    for cp in copies:
+        cp.wait()
+
+
+def write_out(arrays):
+    return pl.pallas_call(
+        write_kernel, out_shape=[jax.ShapeDtypeStruct(a.shape, a.dtype) for a in arrays],
+        in_specs=[pl.BlockSpec(memory_space=pltpu.VMEM)] * len(arrays),
+        out_specs=[pl.BlockSpec(memory_space=pltpu.HBM)] * len(arrays),
+        scratch_shapes=[pltpu.SemaphoreType.DMA((len(arrays),))],
+        compiler_params=pltpu.CompilerParams(vmem_limit_bytes=2**20), name="write_out")(*arrays)
 
 
 def solution(mesh):
@@ -415,9 +423,9 @@
         def rows_first(a):
             return jnp.transpose(a, (1, 2, 0)).reshape(-1, 72)
 
-        dx, dwq, dwk, dwv, dwo, dw_next = backward(
+        dx, dwq, dwk, dwv, dwo, dw_next = write_out(backward(
             x_loc.reshape(T, D), dy_loc.reshape(T, D), rows_first(wq), rows_first(wk), rows_first(wv), wo.reshape(576, 72),
-            g[0], jnp.asarray(rope_tables()))
+            g[0], jnp.asarray(rope_tables())))
 
         def head_first(a, n):
             return jnp.transpose(a.reshape(n, 64, D), (2, 0, 1))[None]

time: 85.6 us -> 70.8 us (0.83)
  local copies, waits for them, and re-layouts: 9.51 us -> 0 us
  Pallas kernels: 75.2 us -> 69.9 us
    unnamed x16 -> x0, local copies, waits for them, and re-layouts: 9.51 us -> none
    pallas_call x1 -> x2, Pallas kernels: 75.2 us -> 69.9 us  [the longest x1 66.6 us: backward(): pl.pallas_call(kernel, out_shape=(buf(T, D), buf(576, D, dtype=F32), buf(...]
where the time goes in v2:
time: 70.8 us; the launch traced here: 70.6 us
  Pallas kernels  69.9 us (99%)
    pallas_call x1, Pallas kernels, backward(): pl.pallas_call(kernel, out_shape=(buf(T, D), buf(576, D, dtype=F32), buf(...  66.6 us
    pallas_call x1, Pallas kernels, write_out(): pl.pallas_call(write_kernel, out_shape=[jax.ShapeDtypeStruct(a.shape, a.d...  3.27 us

profile of v2, /device:TPU:0, one launch (start us, length us, event | category | flops | bytes accessed | tf_op | source)
XLA Modules:
  0.0 70.6 jit_solution(4210217159602029923)
XLA Ops:
  0.6 66.6 %attn_backward_and_sum.1 = (bf16[2048,576]{1,0:T(8,128)(2,1)S(1)}, f32[576,576]{1,0:T(8,128)S(1)}, f32[192,576]{1,0:T(8,128)S(1)}, f32[192,576]{1,0:T(8,128)S(1)...) custom-call(bf16[2048,576]{1,0:T(8,128)(2,1)} %bitcast.32, bf16[2048,576]{1,0:T(8,128)(2,1)} %bitcast.33, ...), custom_call_target="tpu_custom_call" | custom-call | tf_op jit(solution)/shard_map/attn_backward_and_sum/pallas_call | solution.py:382
  67.3 3.3 %write_out.1 = (bf16[2048,576]{1,0:T(8,128)(2,1)}, f32[576,576]{1,0:T(8,128)}, f32[192,576]{1,0:T(8,128)}, f32[192,576]{1,0:T(8,128)}, f32[576,576]{1,0:T(8,128)}, /*index=5*/f32[3,192,576]{2,1,0:T(8,128)}) custom-call(bf16[2048,576]{1,0:T(8,128)(2,1)S(1)} %get-tuple-element.18.refs_0_, f32[576,576]{1,0:T(8,128)S(1)} %get-tuple-element.19.refs_1_, ...), custom_call_target="tpu_custom_call" | custom-call | tf_op jit(solution)/shard_map/write_out/pallas_call | solution.py:410

commit v3 on v2

--- a/solution.py
+++ b/solution.py
@@ -64,20 +64,26 @@
     def blocks(v):
         return jnp.concatenate([jnp.where(first, v, zero), jnp.where(first, zero, v)], axis=0)
 
+    loaded = []
     for g in range(3):
         heads = [64 * (3 * g + r) for r in range(3)]
         q3 = jnp.concatenate([qkvT[h:h + 64, cols] for h in heads], axis=1)
         do3 = jnp.concatenate([doT[h:h + 64, cols] for h in heads], axis=1)
-        kT = qkvT[576 + 64 * g:640 + 64 * g, cols]
-        vT = qkvT[768 + 64 * g:832 + 64 * g, cols]
-        s = nn(kl[g, keys, :], blocks(q3)) * (0.125 * LOG2E)
-        dp = nn(vl[g, keys, :], blocks(do3))
-        s = jnp.where(causal, s, -1e30)
+        loaded.append((heads, q3, do3, nn(kl[g, keys, :], blocks(q3)), nn(vl[g, keys, :], blocks(do3))))
+    soft = []
+    for g in range(3):
+        heads, q3, do3, s, dp = loaded[g]
+        s = jnp.where(causal, s * (0.125 * LOG2E), -1e30)
         e = jnp.exp2(s - jnp.max(s, axis=0, keepdims=True))
         p = e * (1.0 / jnp.sum(e, axis=0, keepdims=True))
         delta = jnp.sum(p * dp, axis=0, keepdims=True)
         ds = (p * (dp - delta) * 0.125).astype(BF)
-        pbd, dsbd = blocks(p.astype(BF)), blocks(ds)
+        soft.append((blocks(p.astype(BF)), blocks(ds)))
+    for g in range(3):
+        heads, q3, do3, s, dp = loaded[g]
+        kT = qkvT[576 + 64 * g:640 + 64 * g, cols]
+        vT = qkvT[768 + 64 * g:832 + 64 * g, cols]
+        pbd, dsbd = soft[g]
         o = nn(vT, pbd).astype(BF)
         dq = nn(kT, dsbd)
         for r in range(3):
@@ -260,13 +266,19 @@
         tr = buf[pl.ds(6 * k, 6)].reshape(288, 384).T
         self.out[k] = jnp.concatenate([tr[0:192], tr[192:384]], axis=1)
 
-    def step(self, t):
-        for off, stage in zip(OFFSETS, (self.s2, self.s3, self.s4, self.s5, self.s6, self.s7)):
-            p = t - off
-
-            @pl.when((p >= 0) & (p < NP))
+    def slot(self, now, length):
+        for k in (7, 6, 5, 4, 3, 2):
+            first = now - START[k] + 10 * PACE
+            p = lax.div(first, PACE) - 10
+
+            @pl.when((lax.div(first + length, PACE) - 10 > p) & (p >= AHEAD[k]) & (p < NP))
             def _():
-                stage(p)
+                getattr(self, f"s{k}")(p)
+
+    def run(self, k, lo, hi):
+        @pl.loop(lo, hi)
+        def _(p):
+            getattr(self, f"s{k}")(p)
 
     def drain(self):
         for n in range(11):
@@ -288,7 +300,9 @@
                 self.c5(p).wait_send()
 
 
-OFFSETS = (0, 3, 5, 7, 10, 13)
+PACE = 7
+START = {2: -47, 3: -26, 4: -11, 5: 2, 6: 20, 7: 46}
+AHEAD = {2: 8, 3: 3, 4: 1, 5: 0, 6: 0, 7: 0}
 
 
 def kernel(x_h, dy_h, wq_h, wk_h, wv_h, wo_h, g, tab, dx, dwq, dwk, dwv, dwo, out,
@@ -310,64 +324,60 @@
     cm.pack()
     for n in range(5):
         cm.wcopy(n).start()
-    cm.convert(0, 3)
-    cm.step(0)
-    cm.convert(3, 5)
-    cm.step(1)
+    cm.convert(0, 2)
+    cm.run(2, 0, 2)
+    cm.convert(2, 6)
     cm.forward(0, 5)
     cm.forward(1, 6)
-    cm.convert(5, 9)
-    cm.step(2)
+    cm.convert(6, 10)
+    cm.run(2, 2, 3)
     cm.forward(2, 7)
     cm.forward(3, 8)
-    cm.convert(9, 13)
-    cm.step(3)
-    cm.convert(13, NP)
-    cm.step(4)
+    cm.convert(10, NP)
+    cm.run(3, 0, 2)
+    cm.run(2, 3, 7)
     cm.forward(5, 9)
     cm.forward(6, 10)
-    cm.step(5)
+    cm.run(3, 2, 3)
+    cm.run(2, 7, 8)
+    cm.run(4, 0, 1)
     for n in (4, 7, 8, 9, 10):
         cm.wcopy(n).wait_recv()
     cm.unpack(w)
     for cp in acts:
         cp.wait()
 
-    def some(i, first, period, of):
-        @pl.when(lax.rem(i, period) < of)
-        def _():
-            cm.step(first + of * lax.div(i, period) + lax.rem(i, period))
-
     @pl.loop(0, 8)
     def _(i):
         project(i, w, x, dy, tab, qkvT, doT, kl, vl)
-        some(i, 6, 3, 2)
+        cm.slot(5 * i, 5)
 
     @pl.loop(0, 16)
     def _(j):
         attend(j, tab, qkvT, doT, kl, vl, oT, dqkvT)
-        some(j, 12, 3, 2)
+        cm.slot(40 + 4 * j, 4)
 
     @pl.loop(0, 8)
     def _(i):
         rows = pl.ds(pl.multiple_of(i * 256, 256), 256)
         dx[rows, :] = tn(dqkvT[:, rows], w[0:960, :]).astype(BF)
-        some(i, 23, 2, 1)
+        cm.slot(104 + 4 * i, 4)
 
     @pl.loop(0, 2)
     def _(h):
         rows = pl.ds(pl.multiple_of(288 * h, 288), 288)
         dwq[rows, :] = nn(dqkvT[rows, :], x[...])
+        cm.slot(136 + 12 * h, 6)
         dwo[rows, :] = nn(oT[rows, :], dy[...])
-        cm.step(27 + h)
+        cm.slot(142 + 12 * h, 6)
 
     dkv = nn(dqkvT[576:960, :], x[...])
     dwk[...] = dkv[0:192]
     dwv[...] = dkv[192:384]
 
-    @pl.loop(29, NP + OFFSETS[-1])
-    def _(t):
-        cm.step(t)
+    @pl.loop(0, -(-(START[7] + PACE * NP - 160) // 4))
+    def _(i):
+        cm.slot(160 + 4 * i, 4)
 
     cm.drain()
 

time: 70.8 us -> 66 us (0.932)
  Pallas kernels: 69.9 us -> 65.2 us
    pallas_call x1, Pallas kernels: 66.6 us -> 61.9 us  [backward(): pl.pallas_call(kernel, out_shape=(buf(T, D), buf(576, D, dtype=F32), buf(...]
where the time goes in v3:
time: 66 us; the launch traced here: 65.8 us
  Pallas kernels  65.2 us (99%)
    pallas_call x1, Pallas kernels, backward(): pl.pallas_call(kernel, out_shape=(buf(T, D), buf(576, D, dtype=F32), buf(...  61.9 us
    pallas_call x1, Pallas kernels, write_out(): pl.pallas_call(write_kernel, out_shape=[jax.ShapeDtypeStruct(a.shape, a.d...  3.27 us

profile of v3, /device:TPU:0, one launch (start us, length us, event | category | flops | bytes accessed | tf_op | source)
XLA Modules:
  0.0 65.8 jit_solution(17354827576700457124)
XLA Ops:
  0.6 61.9 %attn_backward_and_sum.1 = (bf16[2048,576]{1,0:T(8,128)(2,1)S(1)}, f32[576,576]{1,0:T(8,128)S(1)}, f32[192,576]{1,0:T(8,128)S(1)}, f32[192,576]{1,0:T(8,128)S(1)...) custom-call(bf16[2048,576]{1,0:T(8,128)(2,1)} %bitcast.32, bf16[2048,576]{1,0:T(8,128)(2,1)} %bitcast.33, ...), custom_call_target="tpu_custom_call" | custom-call | tf_op jit(solution)/shard_map/attn_backward_and_sum/pallas_call | solution.py:392
  62.6 3.3 %write_out.1 = (bf16[2048,576]{1,0:T(8,128)(2,1)}, f32[576,576]{1,0:T(8,128)}, f32[192,576]{1,0:T(8,128)}, f32[192,576]{1,0:T(8,128)}, f32[576,576]{1,0:T(8,128)}, /*index=5*/f32[3,192,576]{2,1,0:T(8,128)}) custom-call(bf16[2048,576]{1,0:T(8,128)(2,1)S(1)} %get-tuple-element.18.refs_0_, f32[576,576]{1,0:T(8,128)S(1)} %get-tuple-element.19.refs_1_, ...), custom_call_target="tpu_custom_call" | custom-call | tf_op jit(solution)/shard_map/write_out/pallas_call | solution.py:420

commit v4 on v3

--- a/solution.py
+++ b/solution.py
@@ -11,6 +11,11 @@
 F32 = jnp.float32
 BF = jnp.bfloat16
 LOG2E = 1.4426950408889634
+PR = 48
+PC = 384
+SCORE = (64, 384)
+QKV = 960
+ROWS = 1536
 
 
 def rope_tables():
@@ -36,13 +41,13 @@
 def project(i, w, x, dy, tab, qkvT, doT, kl, vl):
     rows = pl.ds(pl.multiple_of(i * 256, 256), 256)
     cos, sin = tab[0], tab[1]
-    raw = nt(w[0:960, :], x[rows, :])
+    raw = nt(w[0:QKV, :], x[rows, :])
     for h in range(12):
         a, b = raw[64 * h:64 * h + 32], raw[64 * h + 32:64 * h + 64]
         qkvT[64 * h:64 * h + 32, rows] = (a * cos - b * sin).astype(BF)
         qkvT[64 * h + 32:64 * h + 64, rows] = (b * cos + a * sin).astype(BF)
-    qkvT[768:960, rows] = raw[768:960].astype(BF)
-    doT[:, rows] = nt(w[960:1536, :], dy[rows, :]).astype(BF)
+    qkvT[768:QKV, rows] = raw[768:QKV].astype(BF)
+    doT[:, rows] = nt(w[QKV:ROWS, :], dy[rows, :]).astype(BF)
     for g in range(3):
         for src, dst in ((576, kl), (768, vl)):
             tr = qkvT[src + 64 * g:src + 64 * g + 64, rows].T
@@ -51,39 +56,41 @@
                 dst[g, keys, :] = jnp.concatenate([tr[128 * s:128 * s + 64], tr[128 * s + 64:128 * s + 128]], axis=1)
 
 
-def attend(j, tab, qkvT, doT, kl, vl, oT, dqkvT):
-    cols = pl.ds(pl.multiple_of(j * 128, 128), 128)
-    keys = pl.ds(pl.multiple_of(j * 64, 64), 64)
+def attend(js, tab, qkvT, doT, kl, vl, oT, dqkvT):
     cos, sin = tab[0, :, 0:128], tab[1, :, 0:128]
-    key_i = lax.broadcasted_iota(jnp.int32, (64, 384), 0)
-    lane = lax.broadcasted_iota(jnp.int32, (64, 384), 1)
+    key_i = lax.broadcasted_iota(jnp.int32, SCORE, 0)
+    lane = lax.broadcasted_iota(jnp.int32, SCORE, 1)
     causal = key_i <= lane % 64
     first = lane % 128 < 64
-    zero = jnp.zeros((64, 384), BF)
+    zero = jnp.zeros(SCORE, BF)
 
     def blocks(v):
         return jnp.concatenate([jnp.where(first, v, zero), jnp.where(first, zero, v)], axis=0)
 
     loaded = []
-    for g in range(3):
+    units = [(j, g) for j in js for g in range(3)]
+    for j, g in units:
+        cols = pl.ds(pl.multiple_of(j * 128, 128), 128)
+        keys = pl.ds(pl.multiple_of(j * 64, 64), 64)
         heads = [64 * (3 * g + r) for r in range(3)]
         q3 = jnp.concatenate([qkvT[h:h + 64, cols] for h in heads], axis=1)
         do3 = jnp.concatenate([doT[h:h + 64, cols] for h in heads], axis=1)
         loaded.append((heads, q3, do3, nn(kl[g, keys, :], blocks(q3)), nn(vl[g, keys, :], blocks(do3))))
     soft = []
-    for g in range(3):
-        heads, q3, do3, s, dp = loaded[g]
+    for n in range(len(units)):
+        heads, q3, do3, s, dp = loaded[n]
         s = jnp.where(causal, s * (0.125 * LOG2E), -1e30)
         e = jnp.exp2(s - jnp.max(s, axis=0, keepdims=True))
         p = e * (1.0 / jnp.sum(e, axis=0, keepdims=True))
         delta = jnp.sum(p * dp, axis=0, keepdims=True)
         ds = (p * (dp - delta) * 0.125).astype(BF)
         soft.append((blocks(p.astype(BF)), blocks(ds)))
-    for g in range(3):
-        heads, q3, do3, s, dp = loaded[g]
+    for n, (j, g) in enumerate(units):
+        cols = pl.ds(pl.multiple_of(j * 128, 128), 128)
+        heads, q3, do3, s, dp = loaded[n]
         kT = qkvT[576 + 64 * g:640 + 64 * g, cols]
         vT = qkvT[768 + 64 * g:832 + 64 * g, cols]
-        pbd, dsbd = soft[g]
+        pbd, dsbd = soft[n]
         o = nn(vT, pbd).astype(BF)
         dq = nn(kT, dsbd)
         for r in range(3):
@@ -188,7 +195,7 @@
             cp.wait()
         slot = lax.rem(p, 4)
         for q in range(4):
-            top = self.gf[slot, 0:48, 384 * q:384 * q + 384].astype(BF)
+            top = self.gf[slot, 0:PR, PC * q:384 * q + 384].astype(BF)
             bot = self.gf[slot, 48:96, 384 * q:384 * q + 384].astype(BF)
             for cc in range(2):
                 lanes = slice(192 * cc, 192 * cc + 192)
@@ -268,12 +275,9 @@
 
     def slot(self, now, length):
         for k in (7, 6, 5, 4, 3, 2):
-            first = now - START[k] + 10 * PACE
-            p = lax.div(first, PACE) - 10
-
-            @pl.when((lax.div(first + length, PACE) - 10 > p) & (p >= AHEAD[k]) & (p < NP))
-            def _():
-                getattr(self, f"s{k}")(p)
+            first = now - START[k] + 20 * PACE[k]
+            lo = lax.max(lax.div(first, PACE[k]) - 20, AHEAD[k])
+            self.run(k, lo, lax.min(lax.div(first + length, PACE[k]) - 20, NP))
 
     def run(self, k, lo, hi):
         @pl.loop(lo, hi)
@@ -300,84 +304,103 @@
                 self.c5(p).wait_send()
 
 
-PACE = 7
-START = {2: -47, 3: -26, 4: -11, 5: 2, 6: 20, 7: 46}
-AHEAD = {2: 8, 3: 3, 4: 1, 5: 0, 6: 0, 7: 0}
-
-
-def kernel(x_h, dy_h, wq_h, wk_h, wv_h, wo_h, g, tab, dx, dwq, dwk, dwv, dwo, out,
-           x, dy, w, qkvT, doT, kl, vl, oT, dqkvT, insem, *bufs):
+START = {2: -56, 3: -28, 4: -14, 5: -2, 6: 16, 7: 42}
+PACE = {2: 7, 3: 7, 4: 7, 5: 7, 6: 7, 7: 7}
+AHEAD = {2: 8, 3: 4, 4: 2, 5: 0, 6: 0, 7: 0}
+SLICE = {"project": 5, "attend": 4, "dx": 7, "dw": 6, "tail": 4}
+
+
+def kernel(x_h, dy_h, wq_h, wk_h, wv_h, wo_h, g, tab_h, dx, dwq, dwk, dwv, dwo, out,
+           x, dy, w, qkvT, doT, kl, vl, oT, dqkvT, tab, insem, *bufs):
     cm = Comm(g, out, *bufs)
     loads = [pltpu.make_async_copy(src, cm.wl.at[lo:lo + n, :], insem.at[i])
-             for i, (src, lo, n) in enumerate(((wq_h, 0, 576), (wk_h, 576, 192), (wv_h, 768, 192), (wo_h, 960, 576)))]
+             for i, (src, lo, n) in enumerate(((wq_h, 0, 576), (wk_h, 576, 192), (wv_h, 768, 192), (wo_h, QKV, 576)))]
     for cp in loads:
         cp.start()
     for p in range(4):
         for cp in cm.load(p):
             cp.start()
-    acts = [pltpu.make_async_copy(x_h, x, insem.at[4]), pltpu.make_async_copy(dy_h, dy, insem.at[5])]
+    acts = [pltpu.make_async_copy(x_h, x, insem.at[4]), pltpu.make_async_copy(dy_h, dy, insem.at[5]),
+            pltpu.make_async_copy(tab_h, tab, insem.at[6])]
     for cp in acts:
         cp.start()
     cm.barrier()
     for cp in loads:
         cp.wait()
     cm.pack()
-    for n in range(5):
-        cm.wcopy(n).start()
+    cm.wcopy(0).start()
+    cm.wcopy(1).start()
+    cm.wcopy(4).start()
     cm.convert(0, 2)
     cm.run(2, 0, 2)
-    cm.convert(2, 6)
+    cm.wcopy(2).start()
+    cm.wcopy(3).start()
+    cm.convert(2, 4)
     cm.forward(0, 5)
     cm.forward(1, 6)
-    cm.convert(6, 10)
-    cm.run(2, 2, 3)
+    cm.convert(4, 8)
+    cm.run(2, 2, 4)
     cm.forward(2, 7)
     cm.forward(3, 8)
-    cm.convert(10, NP)
+    cm.convert(8, 12)
     cm.run(3, 0, 2)
-    cm.run(2, 3, 7)
+    cm.convert(12, 18)
+    cm.run(2, 4, 6)
     cm.forward(5, 9)
     cm.forward(6, 10)
-    cm.run(3, 2, 3)
-    cm.run(2, 7, 8)
-    cm.run(4, 0, 1)
+    cm.run(4, 0, 2)
+    cm.run(3, 2, 4)
+    cm.run(2, 6, 8)
     for n in (4, 7, 8, 9, 10):
         cm.wcopy(n).wait_recv()
     cm.unpack(w)
     for cp in acts:
         cp.wait()
 
+    long = SLICE["project"]
+
     @pl.loop(0, 8)
     def _(i):
         project(i, w, x, dy, tab, qkvT, doT, kl, vl)
-        cm.slot(5 * i, 5)
+        cm.slot(long * i, long)
+
+    at1 = 8 * long
+    long1 = SLICE["attend"]
 
     @pl.loop(0, 16)
     def _(j):
-        attend(j, tab, qkvT, doT, kl, vl, oT, dqkvT)
-        cm.slot(40 + 4 * j, 4)
-
-    @pl.loop(0, 8)
+        attend((j,), tab, qkvT, doT, kl, vl, oT, dqkvT)
+        cm.slot(at1 + long1 * j, long1)
+
+    at2 = at1 + 16 * long1
+    long2 = SLICE["dx"]
+
+    @pl.loop(0, 4)
     def _(i):
-        rows = pl.ds(pl.multiple_of(i * 256, 256), 256)
-        dx[rows, :] = tn(dqkvT[:, rows], w[0:960, :]).astype(BF)
-        cm.slot(104 + 4 * i, 4)
+        rows = pl.ds(pl.multiple_of(i * 512, 512), 512)
+        dx[rows, :] = tn(dqkvT[:, rows], w[0:QKV, :]).astype(BF)
+        cm.slot(at2 + long2 * i, long2)
+
+    at3 = at2 + 4 * long2
+    long3 = SLICE["dw"]
 
     @pl.loop(0, 2)
     def _(h):
         rows = pl.ds(pl.multiple_of(288 * h, 288), 288)
         dwq[rows, :] = nn(dqkvT[rows, :], x[...])
-        cm.slot(136 + 12 * h, 6)
+        cm.slot(at3 + 2 * long3 * h, long3)
         dwo[rows, :] = nn(oT[rows, :], dy[...])
-        cm.slot(142 + 12 * h, 6)
-
-    dkv = nn(dqkvT[576:960, :], x[...])
+        cm.slot(at3 + 2 * long3 * h + long3, long3)
+
+    dkv = nn(dqkvT[576:QKV, :], x[...])
     dwk[...] = dkv[0:192]
     dwv[...] = dkv[192:384]
-
-    @pl.loop(0, -(-(START[7] + PACE * NP - 160) // 4))
+    at4 = at3 + 4 * long3
+    long4 = SLICE["tail"]
+
+    @pl.loop(0, -(-(START[7] + PACE[7] * NP - at4) // long4))
     def _(i):
-        cm.slot(160 + 4 * i, 4)
+        cm.slot(at4 + long4 * i, long4)
 
     cm.drain()
 
@@ -393,13 +416,13 @@
         kernel,
         out_shape=(buf(T, D), buf(576, D, dtype=F32), buf(192, D, dtype=F32), buf(192, D, dtype=F32), buf(576, D, dtype=F32),
                    buf(3, 192, D, dtype=F32)),
-        in_specs=[hbm] * 7 + [vm], out_specs=[vm] * 6,
+        in_specs=[hbm] * 8, out_specs=[vm] * 6,
         scratch_shapes=[
-            buf(T, D), buf(T, D), buf(1536, D), buf(960, T), buf(576, T), buf(3, 1024, 128), buf(3, 1024, 128), buf(576, T),
-            buf(960, T), dma((6,)),
-            buf(1536, 72), buf(8, 96, 1152), buf(4, 96, 1536, dtype=F32), buf(NP, 2, 4, 48, 384), buf(NP, 4, 48, 384),
-            buf(NP, 2, 2, 48, 384), buf(NP, 2, 48, 384), buf(NP, 2, 48, 384), buf(NP, 48, 384), buf(NP, 48, 384),
-            buf(NP, 48, 384), buf(NP, 48, 384, dtype=F32), buf(NP, 48, 384, dtype=F32), buf(NP, 48, 384, dtype=F32),
+            buf(T, D), buf(T, D), buf(ROWS, D), buf(QKV, T), buf(576, T), buf(3, 1024, 128), buf(3, 1024, 128), buf(576, T),
+            buf(QKV, T), buf(2, 32, 256, dtype=F32), dma((7,)),
+            buf(ROWS, 72), buf(8, 96, 1152), buf(4, 96, ROWS, dtype=F32), buf(NP, 2, 4, PR, PC), buf(NP, 4, PR, PC),
+            buf(NP, 2, 2, PR, PC), buf(NP, 2, PR, PC), buf(NP, 2, PR, PC), buf(NP, PR, PC), buf(NP, PR, PC),
+            buf(NP, PR, PC), buf(NP, PR, PC, dtype=F32), buf(NP, PR, PC, dtype=F32), buf(NP, PR, PC, dtype=F32),
             dma((6, NP)), dma((6, NP)), dma((11,)), dma((11,)), dma((2, NP))],
         compiler_params=pltpu.CompilerParams(vmem_limit_bytes=50 * 2**20, collective_id=0, has_side_effects=True),
         name="attn_backward_and_sum",

time: 66 us -> 65.1 us (0.986)
  Pallas kernels: 65.2 us -> 64.3 us
    pallas_call x1, Pallas kernels: 61.9 us -> 61 us  [backward(): pl.pallas_call(kernel, out_shape=(buf(T, D), buf(576, D, dtype=F32), buf(...]
where the time goes in v4:
time: 65.1 us; the launch traced here: 64.9 us
  Pallas kernels  64.3 us (99%)
    pallas_call x1, Pallas kernels, backward(): pl.pallas_call(kernel, out_shape=(buf(T, D), buf(576, D, dtype=F32), buf(...  61 us
    pallas_call x1, Pallas kernels, write_out(): pl.pallas_call(write_kernel, out_shape=[jax.ShapeDtypeStruct(a.shape, a.d...  3.27 us

profile of v4, /device:TPU:0, one launch (start us, length us, event | category | flops | bytes accessed | tf_op | source)
XLA Modules:
  0.0 64.9 jit_solution(10593330431423401675)
XLA Ops:
  0.6 61.0 %attn_backward_and_sum.1 = (bf16[2048,576]{1,0:T(8,128)(2,1)S(1)}, f32[576,576]{1,0:T(8,128)S(1)}, f32[192,576]{1,0:T(8,128)S(1)}, f32[192,576]{1,0:T(8,128)S(1)...) custom-call(bf16[2048,576]{1,0:T(8,128)(2,1)} %bitcast.32, bf16[2048,576]{1,0:T(8,128)(2,1)} %bitcast.33, ...), custom_call_target="tpu_custom_call" | custom-call | tf_op jit(solution)/shard_map/attn_backward_and_sum/pallas_call | solution.py:415
  61.6 3.3 %write_out.1 = (bf16[2048,576]{1,0:T(8,128)(2,1)}, f32[576,576]{1,0:T(8,128)}, f32[192,576]{1,0:T(8,128)}, f32[192,576]{1,0:T(8,128)}, f32[576,576]{1,0:T(8,128)}, /*index=5*/f32[3,192,576]{2,1,0:T(8,128)}) custom-call(bf16[2048,576]{1,0:T(8,128)(2,1)S(1)} %get-tuple-element.18.refs_0_, f32[576,576]{1,0:T(8,128)S(1)} %get-tuple-element.19.refs_1_, ...), custom_call_target="tpu_custom_call" | custom-call | tf_op jit(solution)/shard_map/write_out/pallas_call | solution.py:443
